TPU v7x, 32 devices: a whole 2x2x4 slice. The times are simulated.
32 devices in a mesh: fsdp: 4 (over y, x), ep: 8 (over z, core).
Axes of the slice: x: 2, y: 2, z: 4, core: 2. Of those that a mesh axis runs over, the one named last changes fastest.
Arguments:
- hidden_in: bfloat16 [8192, 2048], P(('fsdp', 'ep')), may hold values from -6 to 6
- norm_gain: float32 [2048], replicated, may hold values from 0.25 to 1.75
- expert_ids: int32 [8192, 8], P(('fsdp', 'ep')), may hold values from 0 to 15, all different within a row; in each aligned block of 256 rows (0 to 255, 256 to 511, ...) at most 160 rows name the same one
- expert_probs: float32 [8192, 8], P(('fsdp', 'ep')), may hold values from 0.05 to 0.25
- gate_proj: bfloat16 [16, 2048, 768], P('ep', 'fsdp'), may hold values from -0.125 to 0.125
- up_proj: bfloat16 [16, 2048, 768], P('ep', 'fsdp'), may hold values from -0.125 to 0.125
- down_proj: bfloat16 [16, 768, 2048], P('ep', None, 'fsdp'), may hold values from -0.21875 to 0.21875
Outputs:
- moe_out: bfloat16 [8192, 2048], P(('fsdp', 'ep'))
Inputs may be any that keep to these rules, and one draw needn't show every extreme that they name: `expert_ids`: within the rows of one device (aligned blocks of 256 rows) each expert id is named by at most 160 rows, and in some blocks one expert by exactly 160; the 8 ids of a row are distinct.
All inputs are finite; a program needn't handle non-finite values.
Results may differ from a plain program's by a relative error of at most 0.0025.
Values may be sent and summed in bfloat16 or wider, within the bound.
A program may use at most 128 MiB of HBM per device.

v0:
```python
import jax
import jax.numpy as jnp
from jax import lax
from jax.sharding import PartitionSpec as P


def rms_norm(hidden_in, norm_gain):
    values = hidden_in.astype(jnp.float32)
    spread = jnp.mean(values * values, axis=-1, keepdims=True)
    return (values * lax.rsqrt(spread + 1e-06) * norm_gain).astype(jnp.bfloat16)


def add_partial(running, inputs, weight_piece, offset):
    columns = lax.dynamic_slice_in_dim(inputs, offset, weight_piece.shape[1], 3)
    return running + jnp.einsum(
        "gecd,edf->gecf", columns, weight_piece, preferred_element_type=jnp.float32
    )


def per_device(hidden_in, norm_gain, expert_ids, expert_probs, gate_proj, up_proj, down_proj):
    tokens_dev, model_width = hidden_in.shape
    top_count = expert_ids.shape[1]
    local_experts = gate_proj.shape[0]
    hidden_width = gate_proj.shape[2]
    groups = lax.axis_size("ep")
    all_experts = local_experts * groups
    capacity = tokens_dev * top_count * 5 // (4 * all_experts)
    normed = rms_norm(hidden_in, norm_gain)
    flat_ids = expert_ids.reshape(-1)
    onehot = (flat_ids[:, None] == jnp.arange(all_experts, dtype=jnp.int32)[None, :]).astype(
        jnp.int32
    )
    before = jnp.cumsum(onehot, axis=0) - onehot
    slot_index = flat_ids * capacity + jnp.sum(before * onehot, axis=1)
    token_of = jnp.arange(tokens_dev * top_count, dtype=jnp.int32) // top_count
    source = jnp.zeros((all_experts * capacity,), jnp.int32).at[slot_index].set(token_of)
    filled = jnp.zeros((all_experts * capacity,), jnp.bool_).at[slot_index].set(True)
    outbound = jnp.where(filled[:, None], normed[source], jnp.zeros((), jnp.bfloat16))
    outbound = outbound.astype(jnp.bfloat16).reshape(groups, local_experts, capacity, model_width)
    inbound = lax.all_to_all(outbound, "ep", split_axis=0, concat_axis=0, tiled=True)
    zero_acc = jnp.zeros((groups, local_experts, capacity, hidden_width), jnp.float32)

    def fold_one(running, weight_piece, offset):
        return add_partial(running, inbound, weight_piece, offset)

    gate_sum = fold_one(
        zero_acc,
        jax.tree.map(lambda part: lax.all_gather(part, "fsdp", axis=1, tiled=True), gate_proj),
        jnp.int32(0),
    )
    up_sum = fold_one(
        zero_acc,
        jax.tree.map(lambda part: lax.all_gather(part, "fsdp", axis=1, tiled=True), up_proj),
        jnp.int32(0),
    )
    activated = (jax.nn.silu(gate_sum) * up_sum).astype(jnp.bfloat16)

    def project(weight_piece):
        return jnp.einsum(
            "gecf,efd->gecd", activated, weight_piece, preferred_element_type=jnp.float32
        ).astype(jnp.bfloat16)

    result = project(lax.all_gather(down_proj, "fsdp", axis=2, tiled=True))
    returned = lax.all_to_all(result, "ep", split_axis=0, concat_axis=0, tiled=True)
    flat_out = returned.reshape(all_experts * capacity, model_width)
    picked = flat_out[slot_index].reshape(tokens_dev, top_count, model_width).astype(jnp.float32)
    combined = jnp.sum(picked * expert_probs[:, :, None], axis=1)
    return combined.astype(jnp.bfloat16)


def solution(mesh):
    return jax.shard_map(
        per_device,
        mesh=mesh,
        in_specs=(
            P(("fsdp", "ep"), None),
            P(),
            P(("fsdp", "ep"), None),
            P(("fsdp", "ep"), None),
            P("ep", "fsdp", None),
            P("ep", "fsdp", None),
            P("ep", None, "fsdp"),
        ),
        out_specs=P(("fsdp", "ep"), None),
        check_vma=False,
    )
```

profile of v0, /device:TPU:0, one launch (start us, length us, event | category | flops | bytes accessed | tf_op | source)
XLA Modules:
  0.0 616.0 jit_solution(7753310625822930992)
XLA Ops:
  6.5 0.0 all-gather.6.cloned.1.call-start
  6.5 0.7 all-gather.6.cloned.1.call-update
  7.3 0.8 copy.17
  8.1 0.1 eq.29
  8.2 0.1 eq.25
  8.3 4.6 reduce-window.6
  12.9 0.4 slice_reduce_fusion
  13.3 0.2 reduce-window.9
  13.5 0.7 broadcast_multiply_fusion
  14.2 0.1 copy.16
  14.3 0.1 mul.55
  14.5 0.1 broadcast_add_fusion
  14.6 0.1 fusion.28
  14.7 8.1 %scatter_custom_fusion.1 = s32[2560]{0:T(1024)S(1)} fusion(s32[2048]{0:T(1024)S(1)} %bitcast.72, s32[2048]{0:T(1024)S(1)} %add_select_fusion, s32[]{:T(128)} %constant.34.clone.1), kind=kCustom, calls=%fused_computation.47 | custom fusion | bytes 10244 | tf_op jit(solution)/shard_map/scatter | solution.py:36
  22.7 9.1 %scatter_custom_fusion = pred[2560]{0:T(1024)(128)(4,1)S(1)} fusion(s32[2048]{0:T(1024)S(1)} %bitcast.73, pred[2048]{0:T(1024)(128)(4,1)S(1)} %broadcast.79, pred[]{:T(512)} %constant.16.clone.1), kind=kCustom, calls=%fused_computation.49 | custom fusion | bytes 2561 | tf_op jit(solution)/shard_map/scatter | solution.py:37
  31.9 0.1 broadcast_in_dim.33
  32.0 1.5 fusion.19
  33.5 1.5 fusion.21
  35.0 10.8 %gather_fusion = bf16[2560,2048]{1,0:T(8,128)(2,1)} fusion(bf16[256,2048]{1,0:T(8,128)(2,1)S(1)} %fusion.21, s32[3072]{0:T(1024)S(1)} %pad_clamp_fusion), kind=kCustom, calls=%fused_computation | custom fusion | bytes 20981760 | tf_op jit(solution)/shard_map/gather | solution.py:38
  45.8 10.0 %broadcast_select_fusion = bf16[8,2,160,2048]{3,2,1,0:T(8,128)(2,1)} fusion(bf16[8,2,160,2048]{3,2,1,0:T(8,128)(2,1)} %bitcast.69, pred[8,2,160]{2,1,0:T(4,128)(4,1)S(1)} %broadcast_in_dim.33), kind=kLoop, calls=%fused_computation.7 | loop fusion | flops 5242880 | bytes 20974080 | tf_op jit(solution)/shard_map/jit(_where)/select_n | solution.py:38
  55.8 6.4 %all-to-all-start = ((bf16[8,2,160,2048]{3,2,1,0:T(8,128)(2,1)}), bf16[8,2,160,2048]{3,2,1,0:T(8,128)(2,1)}, u32[]{:S(2)}, u32[]{:S(2)}) async-start(bf16[8,2,160,2048]{3,2,1,0:T(8,128)(2,1)} %broadcast_select_fusion), calls=%async_computation | async-start | bytes 20971520 | tf_op jit(solution)/shard_map/all_to_all | solution.py:40
  62.2 0.0 all-gather.4.cloned.1.call-start
  62.2 0.7 all-gather.4.cloned.1.call-update
  62.9 0.2 all-gather.8.cloned.1.call-start
  63.1 0.5 all-gather.8.cloned.1.call-update
  63.6 18.1 %all-gather.6.cloned.1.call-done = bf16[2,2048,768]{2,1,0:T(8,128)(2,1)} async-done(((bf16[2,512,768]{2,1,0:T(8,128)(2,1)}), bf16[2,2048,768]{2,1,0:T(8,128)(2,1)}) %all-gather.6.cloned.1.call-update) | async-done | bytes 6291472 | tf_op jit(solution)/shard_map/all_gather | solution.py:53
  81.8 209.3 %all-to-all-done = bf16[8,2,160,2048]{3,2,1,0:T(8,128)(2,1)} async-done(((bf16[8,2,160,2048]{3,2,1,0:T(8,128)(2,1)}), bf16[8,2,160,2048]{3,2,1,0:T(8,128)(2,1)}, u32[]{:S(2)}, u32[]{:S(2)}) %all-to-all-start) | async-done | bytes 10485792 | tf_op jit(solution)/shard_map/all_to_all | solution.py:40
  291.1 14.8 %fusion.1 = f32[2,8,160,768]{3,2,1,0:T(8,128)} fusion(bf16[8,2,160,2048]{3,2,1,0:T(8,128)(2,1)} %all-to-all-done, bf16[2,2048,768]{2,1,0:T(8,128)(2,1)} %all-gather.6.cloned.1.call-done), kind=kOutput, calls=%fused_computation.8 | convolution fusion | flops 8053063680 | bytes 24641536 | tf_op jit(solution)/shard_map/gecd,edf->gecf/dot_general | solution.py:15
  305.8 0.0 all-gather.4.cloned.1.call-done
  305.8 0.0 all-gather.8.cloned.1.call-done
  305.8 25.5 %convert_bitcast_fusion = bf16[8,2,160,2048]{3,2,0,1:T(8,128)(2,1)} fusion(bf16[2,768,2048]{2,1,0:T(8,128)(2,1)} %all-gather.8.cloned.1.call-done, f32[2,8,160,768]{3,2,1,0:T(8,128)} %fusion.1, bf16[2,2048,768]{2,1,0:T(8,128)(2,1)} %all-gather.4.cloned.1.call-done, bf16[8,2,160,2048]{3,2,1,0:T(8,128)(2,1)} %all-to-all-done), kind=kOutput, calls=%fused_computation.6 | convolution fusion | flops 16123166720 | bytes 41418752 | tf_op jit(solution)/shard_map/gecf,efd->gecd/dot_general | solution.py:59
  331.4 10.1 %copy.21 = bf16[8,2,160,2048]{3,2,1,0:T(8,128)(2,1)} copy(bf16[8,2,160,2048]{3,2,0,1:T(8,128)(2,1)} %convert_bitcast_fusion) | data formatting | bytes 20971520 | tf_op jit(solution)/shard_map/convert_element_type | solution.py:61
  341.5 0.0 copy-start
  341.5 5.5 all-to-all-start.1
  347.0 0.0 copy-done
  347.0 0.1 copy.22
  347.2 228.4 %all-to-all-done.1 = bf16[8,2,160,2048]{3,2,1,0:T(8,128)(2,1)} async-done(((bf16[8,2,160,2048]{3,2,1,0:T(8,128)(2,1)}), bf16[8,2,160,2048]{3,2,1,0:T(8,128)(2,1)}, u32[]{:S(2)}, u32[]{:S(2)}) %all-to-all-start.1) | async-done | bytes 10485792 | tf_op jit(solution)/shard_map/all_to_all | solution.py:64
  575.6 21.7 %gather_fusion.1 = bf16[2048,2048]{1,0:T(8,128)(2,1)} fusion(bf16[2560,2048]{1,0:T(8,128)(2,1)} %bitcast.13, s32[2048]{0:T(1024)S(1)} %broadcast_clamp_fusion), kind=kCustom, calls=%fused_computation.1 | custom fusion | bytes 16785408 | tf_op jit(solution)/shard_map/gather | solution.py:66
  597.3 12.2 %fusion = bf16[256,2048]{1,0:T(8,128)(2,1)} fusion(bf16[2048,2048]{1,0:T(8,128)(2,1)} %gather_fusion.1, f32[256,8]{1,0:T(8,128)S(1)} %copy.22), kind=kLoop, calls=%fused_computation.5 | loop fusion | flops 12058624 | bytes 9445376 | tf_op jit(solution)/shard_map/reduce_sum | solution.py:67
  (8 shorter events, 0.1 us)
Async XLA Ops:
  6.5 75.2 %all-gather.6.cloned.1.call-start = ((), (), s32[]{:S(2)}) async-start(), calls=%async_computation.3 | async-start | bytes 7864320 | tf_op jit(solution)/shard_map/all_gather | solution.py:53
  55.8 235.3 %all-to-all-start = ((bf16[8,2,160,2048]{3,2,1,0:T(8,128)(2,1)}), bf16[8,2,160,2048]{3,2,1,0:T(8,128)(2,1)}, u32[]{:S(2)}, u32[]{:S(2)}) async-start(bf16[8,2,160,2048]{3,2,1,0:T(8,128)(2,1)} %broadcast_select_fusion), calls=%async_computation | async-start | bytes 20971520 | tf_op jit(solution)/shard_map/all_to_all | solution.py:40
  62.2 243.7 %all-gather.4.cloned.1.call-start = ((), (), s32[]{:S(2)}) async-start(), calls=%async_computation.2 | async-start | bytes 7864320 | tf_op jit(solution)/shard_map/all_gather | solution.py:48
  62.9 242.9 %all-gather.8.cloned.1.call-start = ((), (), s32[]{:S(2)}) async-start(), calls=%async_computation.4 | async-start | bytes 7864320 | tf_op jit(solution)/shard_map/all_gather | solution.py:63
  341.5 5.5 copy-start
  341.5 234.1 %all-to-all-start.1 = ((bf16[8,2,160,2048]{3,2,1,0:T(8,128)(2,1)}), bf16[8,2,160,2048]{3,2,1,0:T(8,128)(2,1)}, u32[]{:S(2)}, u32[]{:S(2)}) async-start(bf16[8,2,160,2048]{3,2,1,0:T(8,128)(2,1)} %copy.21), calls=%async_computation.1 | async-start | bytes 20971520 | tf_op jit(solution)/shard_map/all_to_all | solution.py:64
Sparse Core Ops, SparseCore 0:
  9.2 72.5 all-gather.5
  83.6 69.8 all-gather.3
  155.3 69.6 all-gather.7
where the time goes:
time: 617 us; the launch traced here: 616 us
  waiting for transfers between devices  458 us (74%)
  local copies, waits for them, and re-layouts  61.7 us (10%)
  matrix products  40.3 us (7%)
  other arithmetic  30.9 us (5%)
  between operations  13.2 us (2%)
  starting transfers between devices  12.1 us (2%)
    all_to_all x1, waiting for transfers between devices, per_device(): lax.all_to_all(result, 'ep', split_axis=0, concat_axis=0, tiled=True)  228 us
    all_to_all x1, waiting for transfers between devices, per_device(): lax.all_to_all(outbound, 'ep', split_axis=0, concat_axis=0, tiled=True)  209 us
    dot_general x1, matrix products, project(): jnp.einsum('gecf,efd->gecd', activated, weight_piece, preferred_element_t...  25.5 us
    gather x1, local copies, waits for them, and re-layouts, per_device(): flat_out[slot_index].reshape(tokens_dev, top_count, model_width)  21.7 us
    all_gather x2, waiting for transfers between devices, per_device(): lax.all_gather(part, 'fsdp', axis=1, tiled=True)  18.1 us
    dot_general x1, matrix products, add_partial(): jnp.einsum('gecd,edf->gecf', columns, weight_piece, preferred_element_typ...  14.8 us
  transfers between devices with their start and end apart: 5, of which 3 were waited for; matrix products, arithmetic and copies ran while one was open for 10% of the time, Pallas kernels for 0%

commit v1 on v0

v1 whole, which is shorter than its diff:
```python
import jax
import jax.numpy as jnp
from jax import lax
from jax.sharding import PartitionSpec as P


def rms_norm(hidden_in, norm_gain):
    values = hidden_in.astype(jnp.float32)
    spread = jnp.mean(values * values, axis=-1, keepdims=True)
    return (values * lax.rsqrt(spread + 1e-06) * norm_gain).astype(jnp.bfloat16)


def per_device(hidden_in, norm_gain, expert_ids, expert_probs, gate_proj, up_proj, down_proj):
    local_experts = gate_proj.shape[0]
    normed = rms_norm(hidden_in, norm_gain)
    all_experts = local_experts * lax.axis_size("ep")
    hot = expert_ids[:, :, None] == jnp.arange(all_experts, dtype=jnp.int32)
    weights = jnp.sum(jnp.where(hot, expert_probs[:, :, None], 0.0), axis=1)
    tokens = lax.all_gather(normed, "ep", axis=0, tiled=True)
    routed = lax.all_to_all(
        weights.reshape(weights.shape[0], lax.axis_size("ep"), local_experts),
        "ep", split_axis=1, concat_axis=0, tiled=True,
    ).reshape(tokens.shape[0], local_experts)
    total = 0.0
    gate_all = lax.all_gather(gate_proj, "fsdp", axis=1, tiled=True)
    up_all = lax.all_gather(up_proj, "fsdp", axis=1, tiled=True)
    down_all = lax.all_gather(down_proj, "fsdp", axis=2, tiled=True)
    for e in range(local_experts):
        gate = jnp.dot(tokens, gate_all[e], preferred_element_type=jnp.float32)
        up = jnp.dot(tokens, up_all[e], preferred_element_type=jnp.float32)
        act = (jax.nn.silu(gate) * up).astype(jnp.bfloat16)
        out = jnp.dot(act, down_all[e], preferred_element_type=jnp.float32).astype(jnp.bfloat16)
        total = total + out.astype(jnp.float32) * routed[:, e, None]
    combined = lax.psum_scatter(total, "ep", scatter_dimension=0, tiled=True)
    return combined.astype(jnp.bfloat16)


def solution(mesh):
    return jax.shard_map(
        per_device,
        mesh=mesh,
        in_specs=(
            P(("fsdp", "ep"), None),
            P(),
            P(("fsdp", "ep"), None),
            P(("fsdp", "ep"), None),
            P("ep", "fsdp", None),
            P("ep", "fsdp", None),
            P("ep", None, "fsdp"),
        ),
        out_specs=P(("fsdp", "ep"), None),
        check_vma=False,
    )
```

time: 617 us -> 532 us (0.86)
  local copies, waits for them, and re-layouts: 61.7 us -> 0.04 us
  matrix products: 40.3 us -> 68.2 us
  waiting for transfers between devices: 458 us -> 432 us
  other arithmetic: 30.9 us -> 6.76 us
  starting transfers between devices: 12.1 us -> 0.16 us
  blocking collectives: 0 us -> 11.8 us
    all_to_all x2 -> x0, waiting for transfers between devices: 438 us -> none  [the longest x1 228 us: per_device(): lax.all_to_all(result, 'ep', split_axis=0, concat_axis=0, tiled=True)]
    all_gather x3 -> x4, waiting for transfers between devices: 18.1 us -> 262 us  [the longest x1 83.1 us: per_device(): tokens = lax.all_gather(normed, 'ep', axis=0, tiled=True)]
    reduce_scatter x0 -> x1, waiting for transfers between devices: none -> 168 us  [per_device(): combined = lax.psum_scatter(total, 'ep', scatter_dimension=0, tiled=True)]
    gather x2 -> x0, local copies, waits for them, and re-layouts: 32.5 us -> none  [the longest x1 21.7 us: per_device(): flat_out[slot_index].reshape(tokens_dev, top_count, model_width)]
    dot_general x2 -> x4, matrix products: 40.3 us -> 68.2 us  [the longest x2 47.9 us: per_device(): jnp.dot(act, down_all[e], preferred_element_type=jnp.float32)]
    scatter x2 -> x0, local copies, waits for them, and re-layouts: 17.2 us -> none  [the longest x1 9.11 us: per_device(): jnp.zeros((all_experts * capacity,), jnp.bool_).at[slot_index].set(True)]
    reduce_sum x2 -> x1, other arithmetic: 12.3 us -> 0.02 us  [per_device(): weights = jnp.sum(jnp.where(hot, expert_probs[:, :, None], 0.0), axis=1)]
    all_to_all x2 -> x0, starting transfers between devices: 11.9 us -> none  [the longest x1 6.39 us: per_device(): lax.all_to_all(outbound, 'ep', split_axis=0, concat_axis=0, tiled=True)]
  transfers between devices with their start and end apart: 5 -> 5, of which waited for: 3 -> 5; matrix products, arithmetic and copies ran while one was open for 10% -> 5% of each run, Pallas kernels for 0% -> 0%
where the time goes in v1:
time: 532 us
  waiting for transfers between devices  432 us (81%)
  matrix products  68.2 us (13%)
  between operations  13.2 us (2%)
  blocking collectives  11.8 us (2%)
  other arithmetic  6.76 us (1%)
    reduce_scatter x1, waiting for transfers between devices, per_device(): combined = lax.psum_scatter(total, 'ep', scatter_dimension=0, tiled=True)  168 us
    all_gather x1, waiting for transfers between devices, per_device(): tokens = lax.all_gather(normed, 'ep', axis=0, tiled=True)  83.1 us
    all_gather x1, waiting for transfers between devices, per_device(): down_all = lax.all_gather(down_proj, 'fsdp', axis=2, tiled=True)  71.4 us
    all_gather x1, waiting for transfers between devices, per_device(): gate_all = lax.all_gather(gate_proj, 'fsdp', axis=1, tiled=True)  57.1 us
    all_gather x1, waiting for transfers between devices, per_device(): up_all = lax.all_gather(up_proj, 'fsdp', axis=1, tiled=True)  50.4 us
    dot_general x2, matrix products, per_device(): jnp.dot(act, down_all[e], preferred_element_type=jnp.float32)  47.9 us
    dot_general x2, matrix products, per_device(): gate = jnp.dot(tokens, gate_all[e], preferred_element_type=jnp.float32)  20.3 us
    all_to_all x1, blocking collectives, per_device(): lax.all_to_all(weights.reshape(weights.shape[0], lax.axis_size('ep'), loc...  11.8 us
  transfers between devices with their start and end apart: 5, of which 5 were waited for; matrix products, arithmetic and copies ran while one was open for 5% of the time, Pallas kernels for 0%

profile of v1, /device:TPU:0, one launch (start us, length us, event | category | flops | bytes accessed | tf_op | source)
XLA Modules:
  0.0 532.2 jit_solution(4729882364466384271)
XLA Ops:
  6.5 0.0 copy-start
  6.5 0.0 copy-start.1
  6.5 0.0 all-gather.7.cloned.1.call-start
  6.5 0.7 all-gather.7.cloned.1.call-update
  7.3 0.0 all-gather.5.cloned.1.call-start
  7.3 1.5 fusion.5
  8.8 2.5 fusion.7
  11.3 0.0 all-gather.5.cloned.1.call-update
  11.4 0.0 all-gather.9.cloned.1.call-start
  11.4 0.7 all-gather.9.cloned.1.call-update
  12.1 0.0 all-gather.11.cloned.1.call-start
  12.1 0.5 all-gather.11.cloned.1.call-update
  12.7 0.0 reduce-scatter.2.cloned.1.call-start
  12.7 0.0 copy-done
  12.7 0.0 copy-done.1
  12.8 11.8 %all_to_all.15 = f32[256,8,2]{0,2,1:T(2,128)S(1)} all-to-all(f32[256,8,2]{0,2,1:T(2,128)S(1)} %reshape.18), channel_id=1, replica_groups=mesh['fsdp'=4,'ep'=8] {'ep'}, dimensions={1} | all-to-all | bytes 32768 | tf_op jit(solution)/shard_map/all_to_all | solution.py:20
  24.6 57.1 %all-gather.7.cloned.1.call-done = bf16[2,2048,768]{2,1,0:T(8,128)(2,1)} async-done(((bf16[2,512,768]{2,1,0:T(8,128)(2,1)}), bf16[2,2048,768]{2,1,0:T(8,128)(2,1)}) %all-gather.7.cloned.1.call-update) | async-done | bytes 6291472 | tf_op jit(solution)/shard_map/all_gather | solution.py:25
  81.8 83.1 %all-gather.5.cloned.1.call-done = bf16[2048,2048]{1,0:T(8,128)(2,1)} async-done(((bf16[256,2048]{1,0:T(8,128)(2,1)}), bf16[2048,2048]{1,0:T(8,128)(2,1)}) %all-gather.5.cloned.1.call-update) | async-done | bytes 8388624 | tf_op jit(solution)/shard_map/all_gather | solution.py:19
  164.8 0.0 copy-start.2
  164.8 0.0 copy-start.3
  164.8 11.8 %fusion.1 = f32[2048,768]{1,0:T(8,128)} fusion(bf16[2048,2048]{1,0:T(8,128)(2,1)} %all-gather.5.cloned.1.call-done, bf16[2,2048,768]{2,1,0:T(8,128)(2,1)} %all-gather.7.cloned.1.call-done), kind=kOutput, calls=%fused_computation.7 | convolution fusion | flops 6442450944 | bytes 17825792 | tf_op jit(solution)/shard_map/dot_general | solution.py:29
  176.6 0.0 copy-done.2
  176.6 0.0 copy-done.3
  176.6 8.5 %fusion.2 = f32[2048,768]{1,0:T(8,128)} fusion(bf16[2048,2048]{1,0:T(8,128)(2,1)S(1)} %copy-done.2, bf16[2,2048,768]{2,1,0:T(8,128)(2,1)S(1)} %copy-done.3), kind=kOutput, calls=%fused_computation.11 | convolution fusion | flops 6442450944 | bytes 17825792 | tf_op jit(solution)/shard_map/dot_general | solution.py:29
  185.2 50.4 %all-gather.9.cloned.1.call-done = bf16[2,2048,768]{2,1,0:T(8,128)(2,1)} async-done(((bf16[2,512,768]{2,1,0:T(8,128)(2,1)}), bf16[2,2048,768]{2,1,0:T(8,128)(2,1)}) %all-gather.9.cloned.1.call-update) | async-done | bytes 6291472 | tf_op jit(solution)/shard_map/all_gather | solution.py:26
  235.5 71.4 %all-gather.11.cloned.1.call-done = bf16[2,768,2048]{2,1,0:T(8,128)(2,1)} async-done(((bf16[2,768,512]{2,1,0:T(8,128)(2,1)}), bf16[2,768,2048]{2,1,0:T(8,128)(2,1)}) %all-gather.11.cloned.1.call-update) | async-done | bytes 6291472 | tf_op jit(solution)/shard_map/all_gather | solution.py:27
  306.9 22.1 %fusion = bf16[2048,2048]{1,0:T(8,128)(2,1)} fusion(f32[2048,768]{1,0:T(8,128)} %fusion.2, bf16[2048,2048]{1,0:T(8,128)(2,1)} %all-gather.5.cloned.1.call-done, bf16[2,768,2048]{2,1,0:T(8,128)(2,1)} %all-gather.11.cloned.1.call-done, bf16[2,2048,768]{2,1,0:T(8,128)(2,1)} %all-gather.9.cloned.1.call-done), kind=kOutput, calls=%fused_computation.3 | convolution fusion | flops 12894339072 | bytes 29360128 | tf_op jit(solution)/shard_map/dot_general | solution.py:32
  329.0 25.8 %multiply_add_fusion = f32[2048,2048]{1,0:T(8,128)} fusion(f32[2048]{0:T(1024)S(1)} %bitcast.35, f32[2048]{0:T(1024)S(1)} %bitcast.34, bf16[2048,2048]{1,0:T(8,128)(2,1)} %fusion, f32[2048,768]{1,0:T(8,128)} %fusion.1, bf16[2048,2048]{1,0:T(8,128)(2,1)} %all-gather.5.cloned.1.call-done, bf16[2,768,2048]{2,1,0:T(8,128)(2,1)} %all-gather.11.cloned.1.call-done, ...), kind=kOutput, calls=%fused_computation | convolution fusion | flops 12919504896 | bytes 46153728 | tf_op jit(solution)/shard_map/dot_general | solution.py:32
  354.8 0.0 reduce-scatter.2.cloned.1.call-update
  354.8 168.1 %reduce-scatter.2.cloned.1.call-done = f32[256,2048]{1,0:T(8,128)} async-done(((f32[2048,2048]{1,0:T(8,128)}), f32[256,2048]{1,0:T(8,128)}) %reduce-scatter.2.cloned.1.call-update) | async-done | bytes 2097168 | tf_op jit(solution)/shard_map/reduce_scatter | solution.py:34
  522.9 2.7 convert_element_type.35
  (4 shorter events, 0.1 us)
Async XLA Ops:
  6.5 6.2 %copy-start = (f32[256,8]{0,1:T(8,128)S(1)}, f32[256,8]{0,1:T(8,128)}, u32[]{:S(2)}) copy-start(f32[256,8]{0,1:T(8,128)} %param.10) | copy-start | bytes 24580
  6.5 6.2 %copy-start.1 = (s32[256,8]{0,1:T(8,128)S(1)}, s32[256,8]{0,1:T(8,128)}, u32[]{:S(2)}) copy-start(s32[256,8]{0,1:T(8,128)} %param.9) | copy-start | bytes 24580
  6.5 75.2 %all-gather.7.cloned.1.call-start = ((), (), s32[]{:S(2)}) async-start(), calls=%async_computation.3 | async-start | bytes 7864320 | tf_op jit(solution)/shard_map/all_gather | solution.py:25
  7.3 157.6 %all-gather.5.cloned.1.call-start = ((), (), s32[]{:S(2)}) async-start(), calls=%async_computation.2 | async-start | bytes 9437184 | tf_op jit(solution)/shard_map/all_gather | solution.py:19
  11.4 224.2 %all-gather.9.cloned.1.call-start = ((), (), s32[]{:S(2)}) async-start(), calls=%async_computation.4 | async-start | bytes 7864320 | tf_op jit(solution)/shard_map/all_gather | solution.py:26
  12.1 294.8 %all-gather.11.cloned.1.call-start = ((), (), s32[]{:S(2)}) async-start(), calls=%async_computation.5 | async-start | bytes 7864320 | tf_op jit(solution)/shard_map/all_gather | solution.py:27
  12.7 510.3 %reduce-scatter.2.cloned.1.call-start = ((), (), s32[]{:S(2)}) async-start(), calls=%async_computation.6 | async-start | bytes 18874368 | tf_op jit(solution)/shard_map/reduce_scatter | solution.py:34
  164.8 11.8 %copy-start.2 = (bf16[2048,2048]{1,0:T(8,128)(2,1)S(1)}, bf16[2048,2048]{1,0:T(8,128)(2,1)}, u32[]{:S(2)}) copy-start(bf16[2048,2048]{1,0:T(8,128)(2,1)} %all-gather.5.cloned.1.call-done) | copy-start | bytes 25165828
  164.8 11.8 %copy-start.3 = (bf16[2,2048,768]{2,1,0:T(8,128)(2,1)S(1)}, bf16[2,2048,768]{2,1,0:T(8,128)(2,1)}, u32[]{:S(2)}) copy-start(bf16[2,2048,768]{2,1,0:T(8,128)(2,1)} %all-gather.7.cloned.1.call-done) | copy-start | bytes 18874372
Sparse Core Ops, SparseCore 0:
  9.2 72.5 all-gather.6
  83.4 81.4 all-gather.4
  166.7 68.7 all-gather.8
  237.2 69.6 all-gather.10
  354.9 167.9 reduce-scatter.1

commit v2 on v1

v2 whole, which is shorter than its diff:
```python
import functools

import jax
import jax.numpy as jnp
from jax import lax
from jax.experimental import pallas as pl
from jax.experimental.pallas import tpu as pltpu
from jax.sharding import PartitionSpec as P


WEIGHT_LIMIT, PROB_LIMIT = 0.21875, 0.25


def rms_norm(hidden_in, norm_gain):
    values = hidden_in.astype(jnp.float32)
    spread = jnp.mean(values * values, axis=-1, keepdims=True)
    return (values * lax.rsqrt(spread + 1e-06) * norm_gain).astype(jnp.bfloat16)


def flip(value, size, bit):
    return lax.ppermute(value, "fsdp", [(i, i ^ bit) for i in range(size)])


def gather_pair(left, right, size):
    if size != 4:
        whole = [lax.all_gather(part, "fsdp", axis=0) for part in (left, right)]
        return [[part[i] for i in range(size)] for part in whole]

    def move(value, bit):
        return flip(value, size, bit)

    left_one, right_two = move(left, 1), move(right, 2)
    left_two, right_one = move(left, 2), move(right, 1)
    left_far, right_far = move(left_two, 1), move(right_one, 2)
    return [left, left_one, left_two, left_far], [right, right_one, right_two, right_far]


def hidden_kernel(count, place, x_ref, *refs):
    gates, ups = refs[:count], refs[count:2 * count]
    act_ref, peak_ref, gate_all, up_all = refs[2 * count:]
    depth = gates[0].shape[0]

    @pl.when(pl.program_id(0) == 0)
    def _():
        for k in range(count):
            rows = pl.ds(pl.multiple_of(place[k] * depth, depth), depth)
            gate_all[rows, :] = gates[k][...]
            up_all[rows, :] = ups[k][...]

    gate = jnp.dot(x_ref[...], gate_all[...], preferred_element_type=jnp.float32)
    up = jnp.dot(x_ref[...], up_all[...], preferred_element_type=jnp.float32)
    act = gate / (1.0 + jnp.exp(-gate)) * up
    act_ref[...] = act.astype(jnp.bfloat16)
    peak = jnp.max(jnp.abs(act), axis=0, keepdims=True)
    peak_ref[...] = jnp.broadcast_to(jnp.max(peak, axis=1, keepdims=True), peak_ref.shape[1:])[None]


def hidden(tokens, gates, ups, place):
    count = len(gates)
    rows, width = tokens.shape
    depth, units = gates[0].shape
    tile = min(512, rows)
    weight_spec = pl.BlockSpec((depth, units), lambda t, place: (0, 0))
    return pl.pallas_call(
        functools.partial(hidden_kernel, count),
        grid_spec=pltpu.PrefetchScalarGridSpec(
            num_scalar_prefetch=1,
            grid=(rows // tile,),
            in_specs=[pl.BlockSpec((tile, width), lambda t, place: (t, 0))]
            + [weight_spec] * (2 * count),
            out_specs=[
                pl.BlockSpec((tile, units), lambda t, place: (t, 0)),
                pl.BlockSpec((1, 8, 128), lambda t, place: (t, 0, 0)),
            ],
            scratch_shapes=[pltpu.VMEM((width, units), jnp.bfloat16)] * 2,
        ),
        out_shape=[
            jax.ShapeDtypeStruct((rows, units), jnp.bfloat16),
            jax.ShapeDtypeStruct((rows // tile, 8, 128), jnp.float32),
        ],
        cost_estimate=pl.CostEstimate(
            flops=4 * rows * width * units,
            bytes_accessed=2 * rows * (width + units),
            transcendentals=rows * units,
        ),
        name="hidden",
    )(place, tokens, *gates, *ups)


def down_kernel(count, *refs):
    acts, shares = refs[:2 * count], refs[2 * count:2 * count + 2]
    weights, outs = refs[2 * count + 2:3 * count + 2], refs[3 * count + 2:]
    for side in range(2):
        total = None
        for e in range(count):
            one = jnp.dot(acts[2 * e + side][...], weights[e][...], preferred_element_type=jnp.float32)
            one = one.astype(jnp.bfloat16).astype(jnp.float32) * shares[side][:, e:e + 1]
            total = one if total is None else total + one
        outs[side][0] = total


def down(acts, routed, pieces, block):
    count = len(acts)
    rows, units = acts[0].shape
    width = pieces[0].shape[1]
    chips = rows // block // 2
    out = jax.ShapeDtypeStruct((chips, block, width), jnp.float32)
    sides = [lambda k: (2 * k, 0), lambda k: (2 * k + 1, 0)]
    return pl.pallas_call(
        functools.partial(down_kernel, count),
        grid=(chips,),
        in_specs=[pl.BlockSpec((block, units), side) for _ in range(count) for side in sides]
        + [pl.BlockSpec((block, count), side) for side in sides]
        + [pl.BlockSpec((units, width), lambda k: (0, 0))] * count,
        out_specs=[pl.BlockSpec((1, block, width), lambda k: (k, 0, 0))] * 2,
        out_shape=[out, out],
        cost_estimate=pl.CostEstimate(
            flops=2 * count * rows * width * units,
            bytes_accessed=2 * count * rows * units + 4 * rows * width,
            transcendentals=0,
        ),
        name="down",
    )(*[act for act in acts for _ in range(2)], routed, routed, *pieces)


def layer(hidden_in, norm_gain, expert_ids, expert_probs, gate_proj, up_proj, down_proj):
    local_experts = gate_proj.shape[0]
    block, width = hidden_in.shape
    groups, shards = lax.axis_size("ep"), lax.axis_size("fsdp")
    chips = groups // 2
    me = lax.axis_index("ep")
    z, core = me // 2, me % 2
    own = lax.axis_index("fsdp")
    sibling = [(i, i ^ 1) for i in range(groups)]

    normed = rms_norm(hidden_in, norm_gain)
    hot = expert_ids[:, :, None] == jnp.arange(local_experts * groups, dtype=jnp.int32)
    weights = jnp.sum(jnp.where(hot, expert_probs[:, :, None], 0.0), axis=1)

    routed_all = lax.all_gather(weights, "ep", axis=0)
    normed, routed_all = lax.optimization_barrier((normed, routed_all))

    def hop(value, step, way):
        first = range(step - 1, chips - 1) if way > 0 else range(1, chips - step + 1)
        pairs = [(2 * i + c, 2 * (i + way) + c) for i in first for c in range(2)]
        return lax.ppermute(value, "ep", pairs)

    up_way, down_way = [normed], [normed]
    for step in range(1, chips):
        up_way.append(hop(up_way[-1], step, 1))
        down_way.append(hop(down_way[-1], step, -1))
    same = [normed] + [
        jnp.where(z >= k, up_way[k], down_way[chips - k]) for k in range(1, chips)
    ]
    other = [lax.ppermute(part, "ep", sibling) for part in same]
    tokens = jnp.concatenate([part for k in range(chips) for part in (same[k], other[k])], axis=0)
    routed_own = lax.dynamic_slice_in_dim(routed_all, me * local_experts, local_experts, 2)
    chip_of = jnp.mod(z - jnp.arange(chips), chips)
    order = jnp.stack([2 * chip_of + core, 2 * chip_of + 1 - core], axis=1).reshape(-1)
    routed = routed_own[order].reshape(groups * block, local_experts)

    if shards == 4:
        place = own ^ jnp.arange(shards, dtype=jnp.int32)
    else:
        place = jnp.arange(shards, dtype=jnp.int32)
    pairs = [gather_pair(gate_proj[e], up_proj[e], shards) for e in range(local_experts)]
    halves = [
        gather_pair(down_proj[e], down_proj[e + 1], shards)
        for e in range(0, local_experts, 2)
    ]
    downs = [part for half in halves for part in half]
    acts, peaks = [], []
    for pair in pairs:
        act, peak = hidden(tokens, *pair, place)
        acts.append(act)
        peaks.append(jnp.max(peak, axis=0))
    level = functools.reduce(jnp.maximum, peaks)
    level = jnp.maximum(level, lax.ppermute(level, "ep", sibling))
    units = acts[0].shape[1]
    level = jnp.maximum(level, 1e-25) * (WEIGHT_LIMIT * PROB_LIMIT * units * 2 * local_experts / 2**15)
    levels = [level] + [
        lax.ppermute(level, "ep", [(i, (i - 2 * k) % groups) for i in range(groups)])
        for k in range(1, chips)
    ]
    shrink = 1.0 / level[0, 0]

    out = jnp.zeros((block, width), jnp.bfloat16)
    depth = down_proj.shape[2]
    sent = []
    for shard in range(shards):
        ready = acts
        if shard > 1:
            ready, sent[shard - 2] = lax.optimization_barrier((acts, sent[shard - 2]))
        mine, theirs = down(ready, routed, [part[shard] for part in downs], block)
        chip_sum = mine + lax.ppermute(theirs, "ep", sibling)
        sent.append((chip_sum[0], [(chip_sum[k] * shrink).astype(jnp.float16) for k in range(1, chips)]))
    for shard in range(shards):
        total, parts = sent[shard]
        for k in range(1, chips):
            back = [(i, (i - 2 * k) % groups) for i in range(groups)]
            part = lax.ppermute(parts[k - 1], "ep", back)
            total = total + part.astype(jnp.float32) * levels[k][0, 0]
        out = lax.dynamic_update_slice(out, total.astype(jnp.bfloat16), (0, place[shard] * depth))
    return out


def solution(mesh):
    return jax.shard_map(
        layer,
        mesh=mesh,
        in_specs=(
            P(("fsdp", "ep"), None),
            P(),
            P(("fsdp", "ep"), None),
            P(("fsdp", "ep"), None),
            P("ep", "fsdp", None),
            P("ep", "fsdp", None),
            P("ep", None, "fsdp"),
        ),
        out_specs=P(("fsdp", "ep"), None),
        check_vma=False,
    )
```

time: 532 us -> 481 us (0.904)
  waiting for transfers between devices: 432 us -> 243 us
  starting transfers between devices: 0.16 us -> 99.1 us
  Pallas kernels: 0 us -> 70.3 us
  matrix products: 68.2 us -> 0 us
  other arithmetic: 6.76 us -> 29 us
  local copies, waits for them, and re-layouts: 0.04 us -> 19.8 us
  between operations: 13.2 us -> 3.61 us
    all_gather x4 -> x0, waiting for transfers between devices: 262 us -> none  [the longest x1 83.1 us: per_device(): tokens = lax.all_gather(normed, 'ep', axis=0, tiled=True)]
    ppermute x0 -> x48, waiting for transfers between devices: none -> 243 us  [the longest x18 116 us: flip(): return lax.ppermute(value, 'fsdp', [(i, i ^ bit) for i in range(size)])]
    reduce_scatter x1 -> x0, waiting for transfers between devices: 168 us -> none  [per_device(): combined = lax.psum_scatter(total, 'ep', scatter_dimension=0, tiled=True)]
    ppermute x0 -> x48, starting transfers between devices: none -> 99.1 us  [the longest x3 43.8 us: layer(): lax.ppermute(level, 'ep', [(i, (i - 2 * k) % groups) for i in range(group...]
    pallas_call x0 -> x6, Pallas kernels: none -> 70.3 us  [the longest x2 38.9 us: hidden(): pl.pallas_call(functools.partial(hidden_kernel, count), grid_spec=pltpu.P...]
    dot_general x4 -> x0, matrix products: 68.2 us -> none  [the longest x2 47.9 us: per_device(): jnp.dot(act, down_all[e], preferred_element_type=jnp.float32)]
    all_gather x0 -> x1, blocking collectives: none -> 15.7 us  [layer(): routed_all = lax.all_gather(weights, 'ep', axis=0)]
    all_to_all x1 -> x0, blocking collectives: 11.8 us -> none  [per_device(): lax.all_to_all(weights.reshape(weights.shape[0], lax.axis_size('ep'), loc...]
  transfers between devices with their start and end apart: 5 -> 48, of which waited for: 5 -> 22; matrix products, arithmetic and copies ran while one was open for 5% -> 7% of each run, Pallas kernels for 0% -> 15%
where the time goes in v2:
time: 481 us
  waiting for transfers between devices  243 us (51%)
  starting transfers between devices  99.1 us (21%)
  Pallas kernels  70.3 us (15%)
  other arithmetic  29 us (6%)
  local copies, waits for them, and re-layouts  19.8 us (4%)
  blocking collectives  15.7 us (3%)
    ppermute x18, waiting for transfers between devices, flip(): return lax.ppermute(value, 'fsdp', [(i, i ^ bit) for i in range(size)])  116 us
    ppermute x6, waiting for transfers between devices, hop(): return lax.ppermute(value, 'ep', pairs)  68.5 us
    ppermute x12, waiting for transfers between devices, layer(): part = lax.ppermute(parts[k - 1], 'ep', back)  55.2 us
    ppermute x3, starting transfers between devices, layer(): lax.ppermute(level, 'ep', [(i, (i - 2 * k) % groups) for i in range(group...  43.8 us
    pallas_call x2, Pallas kernels, hidden(): pl.pallas_call(functools.partial(hidden_kernel, count), grid_spec=pltpu.P...  38.9 us
    pallas_call x4, Pallas kernels, down(): pl.pallas_call(functools.partial(down_kernel, count), grid=(chips,), in_s...  31.3 us
    ppermute x12, starting transfers between devices, layer(): part = lax.ppermute(parts[k - 1], 'ep', back)  23.5 us
    ppermute x18, starting transfers between devices, flip(): return lax.ppermute(value, 'fsdp', [(i, i ^ bit) for i in range(size)])  19.2 us
  transfers between devices with their start and end apart: 48, of which 22 were waited for; matrix products, arithmetic and copies ran while one was open for 7% of the time, Pallas kernels for 15%

profile of v2, /device:TPU:0, one launch (start us, length us, event | category | flops | bytes accessed | tf_op | source)
XLA Modules:
  0.0 480.5 jit_solution(9293444602808084494)
XLA Ops:
  0.0 1.6 fusion
  2.4 15.7 %all-gather = f32[2048,16]{0,1:T(8,128)S(1)} all-gather(f32[256,16]{0,1:T(8,128)S(1)} %select_reduce_fusion), channel_id=2, replica_groups=mesh['fsdp'=4,'ep'=8] {'ep'}, dimensions={0}, use_global_device_ids=true | all-gather | bytes 147456 | tf_op jit(solution)/shard_map/all_gather | solution.py:140
  19.2 1.3 collective-permute-start.2
  20.5 26.0 %collective-permute-done.2 = bf16[256,2048]{1,0:T(8,128)(2,1)S(1)} collective-permute-done((bf16[256,2048]{1,0:T(8,128)(2,1)S(1)}, bf16[256,2048]{1,0:T(8,128)(2,1)S(1)}, u32[]{:S(2)}, u32[]{:S(2)}) %collective-permute-start.2) | collective-permute-done | bytes 1048608 | tf_op jit(solution)/shard_map/ppermute | solution.py:146
  47.8 5.5 %collective-permute-start.1 = (bf16[256,2048]{1,0:T(8,128)(2,1)S(1)}, bf16[256,2048]{1,0:T(8,128)(2,1)}, u32[]{:S(2)}, u32[]{:S(2)}) collective-permute-start(bf16[256,2048]{1,0:T(8,128)(2,1)S(1)} %fusion.2), channel_id=1, source_target_pairs={{0,2},{1,3},{2,4},{3,5},{4,6},{5,7},{8,10},{9,11},{10,12},{11,13},... | collective-permute-start | bytes 3145736 | tf_op jit(solution)/shard_map/ppermute | solution.py:146
  53.3 19.5 %collective-permute-done.3 = bf16[256,2048]{1,0:T(8,128)(2,1)S(1)} collective-permute-done((bf16[256,2048]{1,0:T(8,128)(2,1)S(1)}, bf16[256,2048]{1,0:T(8,128)(2,1)S(1)}, u32[]{:S(2)}, u32[]{:S(2)}) %collective-permute-start.3) | collective-permute-done | bytes 1048608 | tf_op jit(solution)/shard_map/ppermute | solution.py:146
  72.9 1.3 collective-permute-start.4
  74.3 1.3 constant_dynamic-update-slice_fusion.6
  75.6 23.0 %collective-permute-done.4 = bf16[256,2048]{1,0:T(8,128)(2,1)} collective-permute-done((bf16[256,2048]{1,0:T(8,128)(2,1)S(1)}, bf16[256,2048]{1,0:T(8,128)(2,1)}, u32[]{:S(2)}, u32[]{:S(2)}) %collective-permute-start.4) | collective-permute-done | bytes 1048608 | tf_op jit(solution)/shard_map/ppermute | solution.py:146
  98.6 2.6 constant_dynamic-update-slice_fusion.5
  101.1 3.3 copy-done.11
  105.2 2.3 collective-permute-done.5
  107.4 2.3 constant_dynamic-update-slice_fusion.4
  109.8 1.9 constant_dynamic-update-slice_fusion.3
  111.7 1.6 collective-permute-start.8
  114.6 1.5 collective-permute-start.17
  117.2 1.5 constant_dynamic-update-slice_fusion.1
  119.8 1.5 collective-permute-start.19
  122.5 12.8 %collective-permute-done.17.refs_2_ = bf16[512,768]{1,0:T(8,128)(2,1)} collective-permute-done((bf16[512,768]{1,0:T(8,128)(2,1)}, bf16[512,768]{1,0:T(8,128)(2,1)}, u32[]{:S(2)}, u32[]{:S(2)}) %collective-permute-start.17) | collective-permute-done | bytes 786464 | tf_op jit(solution)/shard_map/ppermute | solution.py:21
  135.4 1.5 collective-permute-start.11
  136.9 3.4 collective-permute-done.19.refs_5_
  140.3 1.5 collective-permute-start.13
  141.8 15.4 %collective-permute-done.16.refs_1_ = bf16[512,768]{1,0:T(8,128)(2,1)} collective-permute-done((bf16[512,768]{1,0:T(8,128)(2,1)}, bf16[512,768]{1,0:T(8,128)(2,1)}, u32[]{:S(2)}, u32[]{:S(2)}) %collective-permute-start.16) | collective-permute-done | bytes 786464 | tf_op jit(solution)/shard_map/ppermute | solution.py:21
  157.2 1.5 collective-permute-start.18
  159.8 1.3 copy.14
  163.0 2.4 constant_dynamic-update-slice_fusion.x_ref
  165.9 3.2 collective-permute-done.11.refs_2_
  169.1 1.5 collective-permute-start.14
  170.6 3.4 collective-permute-done.13.refs_5_
  174.0 1.5 collective-permute-start.31
  175.5 15.4 %collective-permute-done.18.refs_3_ = bf16[512,768]{1,0:T(8,128)(2,1)} collective-permute-done((bf16[512,768]{1,0:T(8,128)(2,1)}, bf16[512,768]{1,0:T(8,128)(2,1)}, u32[]{:S(2)}, u32[]{:S(2)}) %collective-permute-start.18) | collective-permute-done | bytes 786464 | tf_op jit(solution)/shard_map/ppermute | solution.py:21
  190.9 1.5 collective-permute-start.12
  192.9 19.5 %hidden.3 = (bf16[2048,768]{1,0:T(8,128)(2,1)}, f32[4,8,128]{2,1,0:T(8,128)}) custom-call(s32[4]{0:T(128)} %iota_xor_fusion.place, bf16[2048,2048]{1,0:T(8,128)(2,1)} %constant_dynamic-update-slice_fusion.x_ref, bf16[512,768]{1,0:T(8,128)(2,1)} %get-tuple-element.81.refs_0_, bf16[512,768]{1,0:T(8,128)(2,1)} %collective-permute-done.16.refs_1_, ...), custom_call_target="tpu_custom_call" | custom-call | flops 12884901888 | bytes 11534336 | tf_op jit(solution)/shard_map/hidden/pallas_call | solution.py:64
  213.0 28.4 %collective-permute-done.12.refs_3_ = bf16[512,768]{1,0:T(8,128)(2,1)} collective-permute-done((bf16[512,768]{1,0:T(8,128)(2,1)}, bf16[512,768]{1,0:T(8,128)(2,1)}, u32[]{:S(2)}, u32[]{:S(2)}) %collective-permute-start.12) | collective-permute-done | bytes 786464 | tf_op jit(solution)/shard_map/ppermute | solution.py:21
  241.4 19.4 %hidden.2 = (bf16[2048,768]{1,0:T(8,128)(2,1)}, f32[4,8,128]{2,1,0:T(8,128)}) custom-call(s32[4]{0:T(128)} %iota_xor_fusion.place, bf16[2048,2048]{1,0:T(8,128)(2,1)} %constant_dynamic-update-slice_fusion.x_ref, bf16[512,768]{1,0:T(8,128)(2,1)} %get-tuple-element.82.refs_0_, bf16[512,768]{1,0:T(8,128)(2,1)} %copy-done.15, ...), custom_call_target="tpu_custom_call" | custom-call | flops 12884901888 | bytes 11534336 | tf_op jit(solution)/shard_map/hidden/pallas_call | solution.py:64
  260.8 7.8 %down.4 = (f32[4,256,512]{2,1,0:T(8,128)}, f32[4,256,512]{2,1,0:T(8,128)}) custom-call(bf16[2048,768]{1,0:T(8,128)(2,1)} %get-tuple-element.53.refs_0_.refs_1_, bf16[2048,768]{1,0:T(8,128)(2,1)} %get-tuple-element.53.refs_0_.refs_1_, bf16[2048,768]{1,0:T(8,128)(2,1)} %get-tuple-element.54.refs_2_.refs_3_, ...), custom_call_target="tpu_custom_call" | custom-call | flops 3221225472 | bytes 10485760 | tf_op jit(solution)/shard_map/down/pallas_call | solution.py:109
  269.7 7.8 %down.5 = (f32[4,256,512]{2,1,0:T(8,128)}, f32[4,256,512]{2,1,0:T(8,128)}) custom-call(bf16[2048,768]{1,0:T(8,128)(2,1)} %get-tuple-element.53.refs_0_.refs_1_, bf16[2048,768]{1,0:T(8,128)(2,1)} %get-tuple-element.53.refs_0_.refs_1_, bf16[2048,768]{1,0:T(8,128)(2,1)} %get-tuple-element.54.refs_2_.refs_3_, ...), custom_call_target="tpu_custom_call" | custom-call | flops 3221225472 | bytes 10485760 | tf_op jit(solution)/shard_map/down/pallas_call | solution.py:109
  278.5 1.5 collective-permute-start.37
  280.1 18.6 %collective-permute-done.36.refs_6_ = bf16[768,512]{1,0:T(8,128)(2,1)} collective-permute-done((bf16[768,512]{1,0:T(8,128)(2,1)}, bf16[768,512]{1,0:T(8,128)(2,1)}, u32[]{:S(2)}, u32[]{:S(2)}) %collective-permute-start.36) | collective-permute-done | bytes 786464 | tf_op jit(solution)/shard_map/ppermute | solution.py:21
  299.2 1.5 collective-permute-start.42
  301.9 2.1 add.138
  305.0 10.6 %collective-permute-done.37.refs_7_ = bf16[768,512]{1,0:T(8,128)(2,1)} collective-permute-done((bf16[768,512]{1,0:T(8,128)(2,1)}, bf16[768,512]{1,0:T(8,128)(2,1)}, u32[]{:S(2)}, u32[]{:S(2)}) %collective-permute-start.37) | collective-permute-done | bytes 786464 | tf_op jit(solution)/shard_map/ppermute | solution.py:21
  315.6 7.8 %down.6 = (f32[4,256,512]{2,1,0:T(8,128)}, f32[4,256,512]{2,1,0:T(8,128)}) custom-call(bf16[2048,768]{1,0:T(8,128)(2,1)} %get-tuple-element.53.refs_0_.refs_1_, bf16[2048,768]{1,0:T(8,128)(2,1)} %get-tuple-element.53.refs_0_.refs_1_, bf16[2048,768]{1,0:T(8,128)(2,1)} %get-tuple-element.54.refs_2_.refs_3_, ...), custom_call_target="tpu_custom_call" | custom-call | flops 3221225472 | bytes 10485760 | tf_op jit(solution)/shard_map/down/pallas_call | solution.py:109
  323.5 2.1 add.143
  326.6 5.0 %collective-permute-done.43.refs_7_ = bf16[768,512]{1,0:T(8,128)(2,1)} collective-permute-done((bf16[768,512]{1,0:T(8,128)(2,1)}, bf16[768,512]{1,0:T(8,128)(2,1)}, u32[]{:S(2)}, u32[]{:S(2)}) %collective-permute-start.43) | collective-permute-done | bytes 786464 | tf_op jit(solution)/shard_map/ppermute | solution.py:21
  331.5 7.8 %down.7 = (f32[4,256,512]{2,1,0:T(8,128)}, f32[4,256,512]{2,1,0:T(8,128)}) custom-call(bf16[2048,768]{1,0:T(8,128)(2,1)} %get-tuple-element.53.refs_0_.refs_1_, bf16[2048,768]{1,0:T(8,128)(2,1)} %get-tuple-element.53.refs_0_.refs_1_, bf16[2048,768]{1,0:T(8,128)(2,1)} %get-tuple-element.54.refs_2_.refs_3_, ...), custom_call_target="tpu_custom_call" | custom-call | flops 3221225472 | bytes 10485760 | tf_op jit(solution)/shard_map/down/pallas_call | solution.py:109
  339.4 43.1 %collective-permute-start.25 = (f32[8,128]{1,0:T(8,128)S(1)}, f32[8,128]{1,0:T(8,128)S(1)}, u32[]{:S(2)}, u32[]{:S(2)}) collective-permute-start(f32[8,128]{1,0:T(8,128)S(1)} %maximum_multiply_fusion), channel_id=1, source_target_pairs={{0,6},{1,7},{2,0},{3,1},{4,2},{5,3},{6,4},{7,5},{8,14},{9,15},{10,... | collective-permute-start | bytes 12296 | tf_op jit(solution)/shard_map/ppermute | solution.py:182
  383.9 4.1 collective-permute-start.24
  393.3 1.6 collective-permute-done.24
  395.0 4.3 collective-permute-start.33
  399.3 20.9 %collective-permute-done.26 = f16[256,512]{1,0:T(8,128)(2,1)} collective-permute-done((f16[256,512]{1,0:T(8,128)(2,1)}, f16[256,512]{1,0:T(8,128)(2,1)}, u32[]{:S(2)}, u32[]{:S(2)}) %collective-permute-start.26) | collective-permute-done | bytes 262176 | tf_op jit(solution)/shard_map/ppermute | solution.py:201
  420.4 3.1 fusion.23
  423.5 2.1 add.148
  425.8 3.9 collective-permute-start.39
  430.8 11.8 %collective-permute-done.34 = f16[256,512]{1,0:T(8,128)(2,1)S(1)} collective-permute-done((f16[256,512]{1,0:T(8,128)(2,1)}, f16[256,512]{1,0:T(8,128)(2,1)S(1)}, u32[]{:S(2)}, u32[]{:S(2)}) %collective-permute-start.34) | collective-permute-done | bytes 262176 | tf_op jit(solution)/shard_map/ppermute | solution.py:201
  442.6 2.0 fusion.24
  445.4 3.9 collective-permute-start.45
  449.2 3.8 collective-permute-start.46
  453.0 1.9 collective-permute-start.47
  455.0 2.4 collective-permute-done.40
  457.4 2.0 fusion.31
  459.4 1.5 collective-permute-done.45
  460.9 16.9 %collective-permute-done.46 = f16[256,512]{1,0:T(8,128)(2,1)S(1)} collective-permute-done((f16[256,512]{1,0:T(8,128)(2,1)S(1)}, f16[256,512]{1,0:T(8,128)(2,1)S(1)}, u32[]{:S(2)}, u32[]{:S(2)}) %collective-permute-start.46) | collective-permute-done | bytes 262176 | tf_op jit(solution)/shard_map/ppermute | solution.py:201
  477.8 2.7 fusion.35
  (121 shorter events, 24.9 us)
Async XLA Ops:
  0.0 18.1 %copy-start = (bf16[256,2048]{1,0:T(8,128)(2,1)S(1)}, bf16[256,2048]{1,0:T(8,128)(2,1)}, u32[]{:S(2)}) copy-start(bf16[256,2048]{1,0:T(8,128)(2,1)} %param.7) | copy-start | bytes 3145732
  19.2 27.3 %collective-permute-start.2 = (bf16[256,2048]{1,0:T(8,128)(2,1)S(1)}, bf16[256,2048]{1,0:T(8,128)(2,1)S(1)}, u32[]{:S(2)}, u32[]{:S(2)}) collective-permute-start(bf16[256,2048]{1,0:T(8,128)(2,1)S(1)} %fusion.2), channel_id=1, source_target_pairs={{2,0},{3,1},{4,2},{5,3},{6,4},{7,5},{10,8},{11,9},{12,10},{13,11},... | collective-permute-start | bytes 3145736 | tf_op jit(solution)/shard_map/ppermute | solution.py:146
  46.5 26.4 %collective-permute-start.3 = (bf16[256,2048]{1,0:T(8,128)(2,1)S(1)}, bf16[256,2048]{1,0:T(8,128)(2,1)S(1)}, u32[]{:S(2)}, u32[]{:S(2)}) collective-permute-start(bf16[256,2048]{1,0:T(8,128)(2,1)S(1)} %collective-permute-done.2), channel_id=1, source_target_pairs={{2,0},{3,1},{4,2},{5,3},{10,8},{11,9},{12,10},{13,11},{18,16},{19,... | collective-permute-start | bytes 3145736 | tf_op jit(solution)/shard_map/ppermute | solution.py:146
  47.7 26.5 %collective-permute-start = (bf16[256,2048]{1,0:T(8,128)(2,1)S(1)}, bf16[256,2048]{1,0:T(8,128)(2,1)}, u32[]{:S(2)}, u32[]{:S(2)}) collective-permute-start(bf16[256,2048]{1,0:T(8,128)(2,1)S(1)} %fusion.2), channel_id=1, source_target_pairs={{0,1},{1,0},{2,3},{3,2},{4,5},{5,4},{6,7},{7,6},{8,9},{9,8},{10,11... | collective-permute-start | bytes 3145736 | tf_op jit(solution)/shard_map/ppermute | solution.py:155
  47.8 27.8 %collective-permute-start.1 = (bf16[256,2048]{1,0:T(8,128)(2,1)S(1)}, bf16[256,2048]{1,0:T(8,128)(2,1)}, u32[]{:S(2)}, u32[]{:S(2)}) collective-permute-start(bf16[256,2048]{1,0:T(8,128)(2,1)S(1)} %fusion.2), channel_id=1, source_target_pairs={{0,2},{1,3},{2,4},{3,5},{4,6},{5,7},{8,10},{9,11},{10,12},{11,13},... | collective-permute-start | bytes 3145736 | tf_op jit(solution)/shard_map/ppermute | solution.py:146
  72.9 25.7 %collective-permute-start.4 = (bf16[256,2048]{1,0:T(8,128)(2,1)S(1)}, bf16[256,2048]{1,0:T(8,128)(2,1)}, u32[]{:S(2)}, u32[]{:S(2)}) collective-permute-start(bf16[256,2048]{1,0:T(8,128)(2,1)S(1)} %collective-permute-done.3), channel_id=1, source_target_pairs={{2,0},{3,1},{10,8},{11,9},{18,16},{19,17},{26,24},{27,25}} | collective-permute-start | bytes 3145736 | tf_op jit(solution)/shard_map/ppermute | solution.py:146
  101.1 3.3 copy-start.11
  104.4 3.0 collective-permute-start.5
  104.4 5.3 %collective-permute-start.6 = (bf16[256,2048]{1,0:T(8,128)(2,1)}, bf16[256,2048]{1,0:T(8,128)(2,1)S(1)}, u32[]{:S(2)}, u32[]{:S(2)}) collective-permute-start(bf16[256,2048]{1,0:T(8,128)(2,1)} %collective-permute-done.1), channel_id=1, source_target_pairs={{2,4},{3,5},{4,6},{5,7},{10,12},{11,13},{12,14},{13,15},{18,20},{1... | collective-permute-start | bytes 3145736 | tf_op jit(solution)/shard_map/ppermute | solution.py:146
  109.8 3.6 copy-start.5
  111.6 4.5 collective-permute-start.7
  111.7 5.5 %collective-permute-start.8 = (bf16[256,2048]{1,0:T(8,128)(2,1)S(1)}, bf16[256,2048]{1,0:T(8,128)(2,1)}, u32[]{:S(2)}, u32[]{:S(2)}) collective-permute-start(bf16[256,2048]{1,0:T(8,128)(2,1)S(1)} %collective-permute-done.6), channel_id=1, source_target_pairs={{4,6},{5,7},{12,14},{13,15},{20,22},{21,23},{28,30},{29,31}} | collective-permute-start | bytes 3145736 | tf_op jit(solution)/shard_map/ppermute | solution.py:146
  114.6 20.7 %collective-permute-start.17 = (bf16[512,768]{1,0:T(8,128)(2,1)}, bf16[512,768]{1,0:T(8,128)(2,1)}, u32[]{:S(2)}, u32[]{:S(2)}) collective-permute-start(bf16[512,768]{1,0:T(8,128)(2,1)} %get-tuple-element.81.refs_0_), channel_id=1, source_target_pairs={{0,16},{8,24},{16,0},{24,8},{1,17},{9,25},{17,1},{25,9},{2,18},{10... | collective-permute-start | bytes 2359304 | tf_op jit(solution)/shard_map/ppermute | solution.py:21
  117.2 1.6 copy-start.6
  118.7 40.0 %collective-permute-start.9 = (bf16[256,2048]{1,0:T(8,128)(2,1)S(1)}, bf16[256,2048]{1,0:T(8,128)(2,1)}, u32[]{:S(2)}, u32[]{:S(2)}) collective-permute-start(bf16[256,2048]{1,0:T(8,128)(2,1)S(1)} %get-tuple-element.58), channel_id=1, source_target_pairs={{0,1},{1,0},{2,3},{3,2},{4,5},{5,4},{6,7},{7,6},{8,9},{9,8},{10,11... | collective-permute-start | bytes 3145736 | tf_op jit(solution)/shard_map/ppermute | solution.py:155
  119.8 43.2 %copy-start.10 = (bf16[512,768]{1,0:T(8,128)(2,1)}, bf16[512,768]{1,0:T(8,128)(2,1)S(1)}, u32[]{:S(2)}) copy-start(bf16[512,768]{1,0:T(8,128)(2,1)S(1)} %get-tuple-element.79.refs_4_) | copy-start | bytes 2359300
  119.8 41.9 %copy-start.7 = (bf16[2,768,512]{2,1,0:T(8,128)(2,1)S(1)}, bf16[2,768,512]{2,1,0:T(8,128)(2,1)}, u32[]{:S(2)}) copy-start(bf16[2,768,512]{2,1,0:T(8,128)(2,1)} %param.13) | copy-start | bytes 4718596
  119.8 20.5 %collective-permute-start.19 = (bf16[512,768]{1,0:T(8,128)(2,1)S(1)}, bf16[512,768]{1,0:T(8,128)(2,1)}, u32[]{:S(2)}, u32[]{:S(2)}) collective-permute-start(bf16[512,768]{1,0:T(8,128)(2,1)S(1)} %get-tuple-element.79.refs_4_), channel_id=1, source_target_pairs={{0,8},{8,0},{16,24},{24,16},{1,9},{9,1},{17,25},{25,17},{2,10},{10... | collective-permute-start | bytes 2359304 | tf_op jit(solution)/shard_map/ppermute | solution.py:21
  121.3 35.9 %collective-permute-start.16 = (bf16[512,768]{1,0:T(8,128)(2,1)}, bf16[512,768]{1,0:T(8,128)(2,1)}, u32[]{:S(2)}, u32[]{:S(2)}) collective-permute-start(bf16[512,768]{1,0:T(8,128)(2,1)} %get-tuple-element.81.refs_0_), channel_id=1, source_target_pairs={{0,8},{8,0},{16,24},{24,16},{1,9},{9,1},{17,25},{25,17},{2,10},{10... | collective-permute-start | bytes 2359304 | tf_op jit(solution)/shard_map/ppermute | solution.py:21
  121.8 43.5 %collective-permute-start.20 = (bf16[512,768]{1,0:T(8,128)(2,1)S(1)}, bf16[512,768]{1,0:T(8,128)(2,1)}, u32[]{:S(2)}, u32[]{:S(2)}) collective-permute-start(bf16[512,768]{1,0:T(8,128)(2,1)S(1)} %get-tuple-element.79.refs_4_), channel_id=1, source_target_pairs={{0,16},{8,24},{16,0},{24,8},{1,17},{9,25},{17,1},{25,9},{2,18},{10... | collective-permute-start | bytes 2359304 | tf_op jit(solution)/shard_map/ppermute | solution.py:21
  135.4 33.7 %collective-permute-start.11 = (bf16[512,768]{1,0:T(8,128)(2,1)}, bf16[512,768]{1,0:T(8,128)(2,1)}, u32[]{:S(2)}, u32[]{:S(2)}) collective-permute-start(bf16[512,768]{1,0:T(8,128)(2,1)} %get-tuple-element.82.refs_0_), channel_id=1, source_target_pairs={{0,16},{8,24},{16,0},{24,8},{1,17},{9,25},{17,1},{25,9},{2,18},{10... | collective-permute-start | bytes 2359304 | tf_op jit(solution)/shard_map/ppermute | solution.py:21
  140.3 33.7 %collective-permute-start.13 = (bf16[512,768]{1,0:T(8,128)(2,1)}, bf16[512,768]{1,0:T(8,128)(2,1)}, u32[]{:S(2)}, u32[]{:S(2)}) collective-permute-start(bf16[512,768]{1,0:T(8,128)(2,1)} %get-tuple-element.80.refs_4_), channel_id=1, source_target_pairs={{0,8},{8,0},{16,24},{24,16},{1,9},{9,1},{17,25},{25,17},{2,10},{10... | collective-permute-start | bytes 2359304 | tf_op jit(solution)/shard_map/ppermute | solution.py:21
  157.2 33.7 %collective-permute-start.18 = (bf16[512,768]{1,0:T(8,128)(2,1)}, bf16[512,768]{1,0:T(8,128)(2,1)}, u32[]{:S(2)}, u32[]{:S(2)}) collective-permute-start(bf16[512,768]{1,0:T(8,128)(2,1)} %collective-permute-done.17.refs_2_), channel_id=1, source_target_pairs={{0,8},{8,0},{16,24},{24,16},{1,9},{9,1},{17,25},{25,17},{2,10},{10... | collective-permute-start | bytes 2359304 | tf_op jit(solution)/shard_map/ppermute | solution.py:21
  158.7 33.7 %collective-permute-start.21 = (bf16[512,768]{1,0:T(8,128)(2,1)}, bf16[512,768]{1,0:T(8,128)(2,1)}, u32[]{:S(2)}, u32[]{:S(2)}) collective-permute-start(bf16[512,768]{1,0:T(8,128)(2,1)} %collective-permute-done.19.refs_5_), channel_id=1, source_target_pairs={{0,16},{8,24},{16,0},{24,8},{1,17},{9,25},{17,1},{25,9},{2,18},{10... | collective-permute-start | bytes 2359304 | tf_op jit(solution)/shard_map/ppermute | solution.py:21
  165.4 47.1 %collective-permute-start.10 = (bf16[512,768]{1,0:T(8,128)(2,1)}, bf16[512,768]{1,0:T(8,128)(2,1)S(1)}, u32[]{:S(2)}, u32[]{:S(2)}) collective-permute-start(bf16[512,768]{1,0:T(8,128)(2,1)} %get-tuple-element.82.refs_0_), channel_id=1, source_target_pairs={{0,8},{8,0},{16,24},{24,16},{1,9},{9,1},{17,25},{25,17},{2,10},{10... | collective-permute-start | bytes 2359304 | tf_op jit(solution)/shard_map/ppermute | solution.py:21
  169.1 44.0 %collective-permute-start.14 = (bf16[512,768]{1,0:T(8,128)(2,1)}, bf16[512,768]{1,0:T(8,128)(2,1)S(1)}, u32[]{:S(2)}, u32[]{:S(2)}) collective-permute-start(bf16[512,768]{1,0:T(8,128)(2,1)} %get-tuple-element.80.refs_4_), channel_id=1, source_target_pairs={{0,16},{8,24},{16,0},{24,8},{1,17},{9,25},{17,1},{25,9},{2,18},{10... | collective-permute-start | bytes 2359304 | tf_op jit(solution)/shard_map/ppermute | solution.py:21
  174.0 94.8 %collective-permute-start.31 = (bf16[768,512]{1,0:T(8,128)(2,1)}, bf16[768,512]{1,0:T(8,128)(2,1)S(1)}, u32[]{:S(2)}, u32[]{:S(2)}) collective-permute-start(bf16[768,512]{1,0:T(8,128)(2,1)} %get-tuple-element.77.refs_7_), channel_id=1, source_target_pairs={{0,8},{8,0},{16,24},{24,16},{1,9},{9,1},{17,25},{25,17},{2,10},{10... | collective-permute-start | bytes 2359304 | tf_op jit(solution)/shard_map/ppermute | solution.py:21
  190.9 50.6 %collective-permute-start.12 = (bf16[512,768]{1,0:T(8,128)(2,1)}, bf16[512,768]{1,0:T(8,128)(2,1)}, u32[]{:S(2)}, u32[]{:S(2)}) collective-permute-start(bf16[512,768]{1,0:T(8,128)(2,1)} %collective-permute-done.11.refs_2_), channel_id=1, source_target_pairs={{0,8},{8,0},{16,24},{24,16},{1,9},{9,1},{17,25},{25,17},{2,10},{10... | collective-permute-start | bytes 2359304 | tf_op jit(solution)/shard_map/ppermute | solution.py:21
  192.4 49.1 %collective-permute-start.15 = (bf16[512,768]{1,0:T(8,128)(2,1)}, bf16[512,768]{1,0:T(8,128)(2,1)}, u32[]{:S(2)}, u32[]{:S(2)}) collective-permute-start(bf16[512,768]{1,0:T(8,128)(2,1)} %collective-permute-done.13.refs_5_), channel_id=1, source_target_pairs={{0,16},{8,24},{16,0},{24,8},{1,17},{9,25},{17,1},{25,9},{2,18},{10... | collective-permute-start | bytes 2359304 | tf_op jit(solution)/shard_map/ppermute | solution.py:21
  212.4 29.0 %copy-start.15 = (bf16[512,768]{1,0:T(8,128)(2,1)}, bf16[512,768]{1,0:T(8,128)(2,1)S(1)}, u32[]{:S(2)}) copy-start(bf16[512,768]{1,0:T(8,128)(2,1)S(1)} %collective-permute-done.10.refs_1_) | copy-start | bytes 2359300
  212.4 56.4 %collective-permute-start.30 = (bf16[768,512]{1,0:T(8,128)(2,1)}, bf16[768,512]{1,0:T(8,128)(2,1)}, u32[]{:S(2)}, u32[]{:S(2)}) collective-permute-start(bf16[768,512]{1,0:T(8,128)(2,1)} %get-tuple-element.78.refs_6_), channel_id=1, source_target_pairs={{0,8},{8,0},{16,24},{24,16},{1,9},{9,1},{17,25},{25,17},{2,10},{10... | collective-permute-start | bytes 2359304 | tf_op jit(solution)/shard_map/ppermute | solution.py:21
  213.0 28.4 %copy-start.16 = (bf16[512,768]{1,0:T(8,128)(2,1)}, bf16[512,768]{1,0:T(8,128)(2,1)S(1)}, u32[]{:S(2)}) copy-start(bf16[512,768]{1,0:T(8,128)(2,1)S(1)} %collective-permute-done.14.refs_6_) | copy-start | bytes 2359300
  268.7 11.4 %copy-start.12 = (f32[4,8,128]{2,1,0:T(8,128)S(1)}, f32[4,8,128]{2,1,0:T(8,128)}, u32[]{:S(2)}) copy-start(f32[4,8,128]{2,1,0:T(8,128)} %get-tuple-element.38) | copy-start | bytes 49156
  268.7 11.4 %copy-start.13 = (f32[4,8,128]{2,1,0:T(8,128)S(1)}, f32[4,8,128]{2,1,0:T(8,128)}, u32[]{:S(2)}) copy-start(f32[4,8,128]{2,1,0:T(8,128)} %get-tuple-element.37) | copy-start | bytes 49156
  268.7 33.2 %copy-start.4 = (f32[4,256,512]{2,1,0:T(8,128)S(1)}, f32[4,256,512]{2,1,0:T(8,128)}, u32[]{:S(2)}) copy-start(f32[4,256,512]{2,1,0:T(8,128)} %get-tuple-element.35) | copy-start | bytes 6291460
  268.7 33.2 %collective-permute-start.22 = (f32[4,256,512]{2,1,0:T(8,128)}, f32[4,256,512]{2,1,0:T(8,128)}, u32[]{:S(2)}, u32[]{:S(2)}) collective-permute-start(f32[4,256,512]{2,1,0:T(8,128)} %get-tuple-element.36), channel_id=1, source_target_pairs={{0,1},{1,0},{2,3},{3,2},{4,5},{5,4},{6,7},{7,6},{8,9},{9,8},{10,11... | collective-permute-start | bytes 6291464 | tf_op jit(solution)/shard_map/ppermute | solution.py:195
  277.5 45.9 %collective-permute-start.32 = (f32[4,256,512]{2,1,0:T(8,128)}, f32[4,256,512]{2,1,0:T(8,128)}, u32[]{:S(2)}, u32[]{:S(2)}) collective-permute-start(f32[4,256,512]{2,1,0:T(8,128)} %get-tuple-element.44), channel_id=1, source_target_pairs={{0,1},{1,0},{2,3},{3,2},{4,5},{5,4},{6,7},{7,6},{8,9},{9,8},{10,11... | collective-permute-start | bytes 6291464 | tf_op jit(solution)/shard_map/ppermute | solution.py:195
  278.0 20.7 %collective-permute-start.36 = (bf16[768,512]{1,0:T(8,128)(2,1)}, bf16[768,512]{1,0:T(8,128)(2,1)}, u32[]{:S(2)}, u32[]{:S(2)}) collective-permute-start(bf16[768,512]{1,0:T(8,128)(2,1)} %get-tuple-element.78.refs_6_), channel_id=1, source_target_pairs={{0,16},{8,24},{16,0},{24,8},{1,17},{9,25},{17,1},{25,9},{2,18},{10... | collective-permute-start | bytes 2359304 | tf_op jit(solution)/shard_map/ppermute | solution.py:21
  278.5 37.1 %collective-permute-start.37 = (bf16[768,512]{1,0:T(8,128)(2,1)}, bf16[768,512]{1,0:T(8,128)(2,1)}, u32[]{:S(2)}, u32[]{:S(2)}) collective-permute-start(bf16[768,512]{1,0:T(8,128)(2,1)} %get-tuple-element.77.refs_7_), channel_id=1, source_target_pairs={{0,16},{8,24},{16,0},{24,8},{1,17},{9,25},{17,1},{25,9},{2,18},{10... | collective-permute-start | bytes 2359304 | tf_op jit(solution)/shard_map/ppermute | solution.py:21
  280.1 19.2 %collective-permute-start.23 = (f32[8,128]{1,0:T(8,128)S(1)}, f32[8,128]{1,0:T(8,128)S(1)}, u32[]{:S(2)}, u32[]{:S(2)}) collective-permute-start(f32[8,128]{1,0:T(8,128)S(1)} %max.12), channel_id=1, source_target_pairs={{0,1},{1,0},{2,3},{3,2},{4,5},{5,4},{6,7},{7,6},{8,9},{9,8},{10,11... | collective-permute-start | bytes 12296 | tf_op jit(solution)/shard_map/ppermute | solution.py:178
  298.7 32.8 %collective-permute-start.43 = (bf16[768,512]{1,0:T(8,128)(2,1)}, bf16[768,512]{1,0:T(8,128)(2,1)}, u32[]{:S(2)}, u32[]{:S(2)}) collective-permute-start(bf16[768,512]{1,0:T(8,128)(2,1)} %copy-done.9), channel_id=1, source_target_pairs={{0,16},{8,24},{16,0},{24,8},{1,17},{9,25},{17,1},{25,9},{2,18},{10... | collective-permute-start | bytes 2359304 | tf_op jit(solution)/shard_map/ppermute | solution.py:21
  299.2 27.4 %collective-permute-start.42 = (bf16[768,512]{1,0:T(8,128)(2,1)}, bf16[768,512]{1,0:T(8,128)(2,1)}, u32[]{:S(2)}, u32[]{:S(2)}) collective-permute-start(bf16[768,512]{1,0:T(8,128)(2,1)} %collective-permute-done.36.refs_6_), channel_id=1, source_target_pairs={{0,8},{8,0},{16,24},{24,16},{1,9},{9,1},{17,25},{25,17},{2,10},{10... | collective-permute-start | bytes 2359304 | tf_op jit(solution)/shard_map/ppermute | solution.py:21
  305.0 18.4 %copy-start.3 = (f32[4,256,512]{2,1,0:T(8,128)S(1)}, f32[4,256,512]{2,1,0:T(8,128)}, u32[]{:S(2)}) copy-start(f32[4,256,512]{2,1,0:T(8,128)} %get-tuple-element.43) | copy-start | bytes 6291460
  323.4 100.0 %collective-permute-start.38 = (f32[4,256,512]{2,1,0:T(8,128)}, f32[4,256,512]{2,1,0:T(8,128)}, u32[]{:S(2)}, u32[]{:S(2)}) collective-permute-start(f32[4,256,512]{2,1,0:T(8,128)} %get-tuple-element.52), channel_id=1, source_target_pairs={{0,1},{1,0},{2,3},{3,2},{4,5},{5,4},{6,7},{7,6},{8,9},{9,8},{10,11... | collective-permute-start | bytes 6291464 | tf_op jit(solution)/shard_map/ppermute | solution.py:195
  326.6 61.9 %copy-start.14 = (s32[4]{0:T(128)S(1)}, s32[4]{0:T(128)}, u32[]{:S(2)}) copy-start(s32[4]{0:T(128)} %iota_xor_fusion.place) | copy-start | bytes 52
  339.4 105.3 %collective-permute-start.44 = (f32[4,256,512]{2,1,0:T(8,128)}, f32[4,256,512]{2,1,0:T(8,128)S(1)}, u32[]{:S(2)}, u32[]{:S(2)}) collective-permute-start(f32[4,256,512]{2,1,0:T(8,128)} %get-tuple-element.56), channel_id=1, source_target_pairs={{0,1},{1,0},{2,3},{3,2},{4,5},{5,4},{6,7},{7,6},{8,9},{9,8},{10,11... | collective-permute-start | bytes 6291464 | tf_op jit(solution)/shard_map/ppermute | solution.py:195
  339.4 44.5 %collective-permute-start.25 = (f32[8,128]{1,0:T(8,128)S(1)}, f32[8,128]{1,0:T(8,128)S(1)}, u32[]{:S(2)}, u32[]{:S(2)}) collective-permute-start(f32[8,128]{1,0:T(8,128)S(1)} %maximum_multiply_fusion), channel_id=1, source_target_pairs={{0,6},{1,7},{2,0},{3,1},{4,2},{5,3},{6,4},{7,5},{8,14},{9,15},{10,... | collective-permute-start | bytes 12296 | tf_op jit(solution)/shard_map/ppermute | solution.py:182
  382.5 5.4 %collective-permute-start.27 = (f32[8,128]{1,0:T(8,128)S(1)}, f32[8,128]{1,0:T(8,128)S(1)}, u32[]{:S(2)}, u32[]{:S(2)}) collective-permute-start(f32[8,128]{1,0:T(8,128)S(1)} %maximum_multiply_fusion), channel_id=1, source_target_pairs={{0,4},{1,5},{2,6},{3,7},{4,0},{5,1},{6,2},{7,3},{8,12},{9,13},{10,... | collective-permute-start | bytes 12296 | tf_op jit(solution)/shard_map/ppermute | solution.py:182
  382.5 5.5 %collective-permute-start.29 = (f32[8,128]{1,0:T(8,128)S(1)}, f32[8,128]{1,0:T(8,128)S(1)}, u32[]{:S(2)}, u32[]{:S(2)}) collective-permute-start(f32[8,128]{1,0:T(8,128)S(1)} %maximum_multiply_fusion), channel_id=1, source_target_pairs={{0,2},{1,3},{2,4},{3,5},{4,6},{5,7},{6,0},{7,1},{8,10},{9,11},{10,... | collective-permute-start | bytes 12296 | tf_op jit(solution)/shard_map/ppermute | solution.py:182
  383.9 11.1 %collective-permute-start.24 = (f16[256,512]{1,0:T(8,128)(2,1)}, f16[256,512]{1,0:T(8,128)(2,1)}, u32[]{:S(2)}, u32[]{:S(2)}) collective-permute-start(f16[256,512]{1,0:T(8,128)(2,1)} %get-tuple-element.40), channel_id=1, source_target_pairs={{0,6},{1,7},{2,0},{3,1},{4,2},{5,3},{6,4},{7,5},{8,14},{9,15},{10,... | collective-permute-start | bytes 786440 | tf_op jit(solution)/shard_map/ppermute | solution.py:201
  387.9 32.3 %collective-permute-start.26 = (f16[256,512]{1,0:T(8,128)(2,1)}, f16[256,512]{1,0:T(8,128)(2,1)}, u32[]{:S(2)}, u32[]{:S(2)}) collective-permute-start(f16[256,512]{1,0:T(8,128)(2,1)} %get-tuple-element.41), channel_id=1, source_target_pairs={{0,4},{1,5},{2,6},{3,7},{4,0},{5,1},{6,2},{7,3},{8,12},{9,13},{10,... | collective-permute-start | bytes 786440 | tf_op jit(solution)/shard_map/ppermute | solution.py:201
  388.0 32.2 %collective-permute-start.28 = (f16[256,512]{1,0:T(8,128)(2,1)}, f16[256,512]{1,0:T(8,128)(2,1)}, u32[]{:S(2)}, u32[]{:S(2)}) collective-permute-start(f16[256,512]{1,0:T(8,128)(2,1)} %get-tuple-element.42), channel_id=1, source_target_pairs={{0,2},{1,3},{2,4},{3,5},{4,6},{5,7},{6,0},{7,1},{8,10},{9,11},{10,... | collective-permute-start | bytes 786440 | tf_op jit(solution)/shard_map/ppermute | solution.py:201
  391.7 31.7 %copy-start.2 = (f32[4,256,512]{2,1,0:T(8,128)S(1)}, f32[4,256,512]{2,1,0:T(8,128)}, u32[]{:S(2)}) copy-start(f32[4,256,512]{2,1,0:T(8,128)} %get-tuple-element.51) | copy-start | bytes 6291460
  395.0 34.7 %collective-permute-start.33 = (f16[256,512]{1,0:T(8,128)(2,1)}, f16[256,512]{1,0:T(8,128)(2,1)S(1)}, u32[]{:S(2)}, u32[]{:S(2)}) collective-permute-start(f16[256,512]{1,0:T(8,128)(2,1)} %get-tuple-element.46), channel_id=1, source_target_pairs={{0,6},{1,7},{2,0},{3,1},{4,2},{5,3},{6,4},{7,5},{8,14},{9,15},{10,... | collective-permute-start | bytes 786440 | tf_op jit(solution)/shard_map/ppermute | solution.py:201
  420.2 22.4 %collective-permute-start.34 = (f16[256,512]{1,0:T(8,128)(2,1)}, f16[256,512]{1,0:T(8,128)(2,1)S(1)}, u32[]{:S(2)}, u32[]{:S(2)}) collective-permute-start(f16[256,512]{1,0:T(8,128)(2,1)} %get-tuple-element.47), channel_id=1, source_target_pairs={{0,4},{1,5},{2,6},{3,7},{4,0},{5,1},{6,2},{7,3},{8,12},{9,13},{10,... | collective-permute-start | bytes 786440 | tf_op jit(solution)/shard_map/ppermute | solution.py:201
  420.2 22.4 %collective-permute-start.35 = (f16[256,512]{1,0:T(8,128)(2,1)S(1)}, f16[256,512]{1,0:T(8,128)(2,1)S(1)}, u32[]{:S(2)}, u32[]{:S(2)}) collective-permute-start(f16[256,512]{1,0:T(8,128)(2,1)S(1)} %get-tuple-element.48), channel_id=1, source_target_pairs={{0,2},{1,3},{2,4},{3,5},{4,6},{5,7},{6,0},{7,1},{8,10},{9,11},{10,... | collective-permute-start | bytes 786440 | tf_op jit(solution)/shard_map/ppermute | solution.py:201
  425.6 19.1 %copy-start.1 = (f32[4,256,512]{2,1,0:T(8,128)S(1)}, f32[4,256,512]{2,1,0:T(8,128)}, u32[]{:S(2)}) copy-start(f32[4,256,512]{2,1,0:T(8,128)} %get-tuple-element.55) | copy-start | bytes 6291460
  425.8 27.2 %collective-permute-start.39 = (f16[256,512]{1,0:T(8,128)(2,1)S(1)}, f16[256,512]{1,0:T(8,128)(2,1)S(1)}, u32[]{:S(2)}, u32[]{:S(2)}) collective-permute-start(f16[256,512]{1,0:T(8,128)(2,1)S(1)} %get-tuple-element.66), channel_id=1, source_target_pairs={{0,6},{1,7},{2,0},{3,1},{4,2},{5,3},{6,4},{7,5},{8,14},{9,15},{10,... | collective-permute-start | bytes 786440 | tf_op jit(solution)/shard_map/ppermute | solution.py:201
  429.7 27.8 %collective-permute-start.40 = (f16[256,512]{1,0:T(8,128)(2,1)S(1)}, f16[256,512]{1,0:T(8,128)(2,1)S(1)}, u32[]{:S(2)}, u32[]{:S(2)}) collective-permute-start(f16[256,512]{1,0:T(8,128)(2,1)S(1)} %get-tuple-element.68), channel_id=1, source_target_pairs={{0,4},{1,5},{2,6},{3,7},{4,0},{5,1},{6,2},{7,3},{8,12},{9,13},{10,... | collective-permute-start | bytes 786440 | tf_op jit(solution)/shard_map/ppermute | solution.py:201
  442.6 14.8 %collective-permute-start.41 = (f16[256,512]{1,0:T(8,128)(2,1)S(1)}, f16[256,512]{1,0:T(8,128)(2,1)S(1)}, u32[]{:S(2)}, u32[]{:S(2)}) collective-permute-start(f16[256,512]{1,0:T(8,128)(2,1)S(1)} %get-tuple-element.67), channel_id=1, source_target_pairs={{0,2},{1,3},{2,4},{3,5},{4,6},{5,7},{6,0},{7,1},{8,10},{9,11},{10,... | collective-permute-start | bytes 786440 | tf_op jit(solution)/shard_map/ppermute | solution.py:201
  445.4 15.5 %collective-permute-start.45 = (f16[256,512]{1,0:T(8,128)(2,1)S(1)}, f16[256,512]{1,0:T(8,128)(2,1)S(1)}, u32[]{:S(2)}, u32[]{:S(2)}) collective-permute-start(f16[256,512]{1,0:T(8,128)(2,1)S(1)} %get-tuple-element.63), channel_id=1, source_target_pairs={{0,6},{1,7},{2,0},{3,1},{4,2},{5,3},{6,4},{7,5},{8,14},{9,15},{10,... | collective-permute-start | bytes 786440 | tf_op jit(solution)/shard_map/ppermute | solution.py:201
  449.2 28.6 %collective-permute-start.46 = (f16[256,512]{1,0:T(8,128)(2,1)S(1)}, f16[256,512]{1,0:T(8,128)(2,1)S(1)}, u32[]{:S(2)}, u32[]{:S(2)}) collective-permute-start(f16[256,512]{1,0:T(8,128)(2,1)S(1)} %get-tuple-element.65), channel_id=1, source_target_pairs={{0,4},{1,5},{2,6},{3,7},{4,0},{5,1},{6,2},{7,3},{8,12},{9,13},{10,... | collective-permute-start | bytes 786440 | tf_op jit(solution)/shard_map/ppermute | solution.py:201
  453.0 24.8 %collective-permute-start.47 = (f16[256,512]{1,0:T(8,128)(2,1)S(1)}, f16[256,512]{1,0:T(8,128)(2,1)S(1)}, u32[]{:S(2)}, u32[]{:S(2)}) collective-permute-start(f16[256,512]{1,0:T(8,128)(2,1)S(1)} %get-tuple-element.64), channel_id=1, source_target_pairs={{0,2},{1,3},{2,4},{3,5},{4,6},{5,7},{6,0},{7,1},{8,10},{9,11},{10,... | collective-permute-start | bytes 786440 | tf_op jit(solution)/shard_map/ppermute | solution.py:201
  459.4 18.4 %copy-start.8 = (bf16[256,2048]{1,0:T(8,128)(2,1)}, bf16[256,2048]{1,0:T(8,128)(2,1)S(1)}, u32[]{:S(2)}) copy-start(bf16[256,2048]{1,0:T(8,128)(2,1)S(1)} %fusion.31) | copy-start | bytes 3145732
  (1 other events, 0.9 us)
